TPU v7x, 256 devices: a whole 4x4x8 slice. The times are simulated.
256 devices in a mesh: shuf: 64 (over y, z, core), rep: 4 (over x).
Axes of the slice: x: 4, y: 4, z: 8, core: 2. Of those that a mesh axis runs over, the one named last changes fastest.
Arguments:
- values: bfloat16 [524288, 1024], P('shuf', 'rep')
- subgroup: int32 [4096], P('shuf'), may hold values from 0 to 31
- owners: int32 [4096, 1], P('shuf'), may hold values from 0 to 63; in each aligned block of 64 rows (0 to 63, 64 to 127, ...) at most 2 rows name the same one
- col_gain: float32 [1024], P('rep'), may hold values from 0.5 to 1.5
- col_bias: float32 [1024], P('rep'), may hold values from -3 to 3
- out_weight: bfloat16 [1024, 1024], P('rep'), may hold values from -0.1875 to 0.1875
Outputs:
- projected: bfloat16 [524288, 1024], P(('shuf', 'rep'))
Inputs may be any that keep to these rules, and one draw needn't show every extreme that they name: `owners`: among the tiles of one index of shuf no owner is named more than 2 times, a bound that some block reaches.
All inputs are finite; a program needn't handle non-finite values.
Results may differ from a plain program's by a relative error of at most 0.015.
Values may be sent and summed in bfloat16 or wider, within the bound.
No kernel may reach another device: no remote copies, remote signals or barrier semaphores. Data moves between devices by JAX's collectives and lax.ppermute only.
A program may use at most 64 MiB of HBM per device.

v0:
```python
import math
import jax
import jax.numpy as jnp
from jax import lax
from jax.sharding import PartitionSpec as P

GRP_DEV = 32
PRIOR = 256


def from_everyone(value, axis):
    peers = lax.axis_size(axis)
    return lax.all_to_all(
        jnp.broadcast_to(value[None], (peers, *value.shape)), axis, 0, 0, tiled=True
    )


def over_copies(value, axis):
    everything = from_everyone(value, axis)
    return jnp.sum(everything, axis=0)


def in_one(arrays, axis):
    flat, at, done = (jnp.concatenate([a.reshape(-1) for a in arrays]), 0, [])
    so_far = over_copies(flat, axis)
    for a in arrays:
        done.append(so_far[at : at + a.size].reshape(a.shape))
        at += a.size
    return tuple(done)


def side_by_side(arrays, axis, split_dim, concat_dim, along):
    widths = [math.prod(a.shape[along:]) for a in arrays]
    both = jnp.concatenate(
        [a.reshape(*a.shape[:along], w) for a, w in zip(arrays, widths)], axis=along
    )
    result = lax.all_to_all(both, axis, split_axis=split_dim, concat_axis=concat_dim, tiled=True)
    pieces = jnp.split(result, [sum(widths[:k]) for k in range(1, len(widths))], axis=along)
    return tuple(
        (b.reshape(*result.shape[:along], *a.shape[along:]) for a, b in zip(arrays, pieces))
    )


def in_one_piece(arrays, axis, split_dim, concat_dim, along):
    ends, at = ([], 0)
    for a in arrays[:-1]:
        at += a.shape[along]
        ends.append(at)
    both = jnp.concatenate(arrays, axis=along)
    return tuple(
        jnp.split(
            lax.all_to_all(both, axis, split_axis=split_dim, concat_axis=concat_dim, tiled=True),
            ends,
            axis=along,
        )
    )


def joined_along(pieces, dim):
    lengths = list(pieces.shape[1:])
    lengths[dim] *= pieces.shape[0]
    return jnp.moveaxis(pieces, 0, dim).reshape(lengths)


def gathered_copies(value, axis, dim):
    return joined_along(from_everyone(value, axis), dim)


def moments(group_sum, group_sq, count, mean_all, square_all):
    weight = (count + float(PRIOR))[:, None]
    center = (group_sum + float(PRIOR) * mean_all) / weight
    second = (group_sq + float(PRIOR) * square_all) / weight
    return (center, lax.rsqrt(second - center * center + 1e-05))


def slot_places(target, capacity, peer_count):
    one_hot = (target[:, None] == jnp.arange(peer_count, dtype=jnp.int32)[None, :]).astype(
        jnp.int32
    )
    position = jnp.sum((jnp.cumsum(one_hot, axis=0) - one_hot) * one_hot, axis=1)
    return target * capacity + position


def on_device(values, subgroup, owners, col_gain, col_bias, out_weight):
    local_rows, local_cols = values.shape
    tile_count = subgroup.shape[0]
    tile_rows = local_rows // tile_count
    peer_count = lax.axis_size("shuf")
    shaped = values.reshape(tile_count, tile_rows, local_cols)
    widened = shaped.astype(jnp.float32)
    tile_sum = jnp.sum(widened, axis=1)
    tile_sq = jnp.sum(widened * widened, axis=1)
    col_sum, col_square = in_one((jnp.sum(tile_sum, axis=0), jnp.sum(tile_sq, axis=0)), "shuf")
    row_count = float(local_rows * peer_count)
    mean_all = col_sum / row_count
    square_all = col_square / row_count
    target = owners[:, 0]
    capacity = max(2, 2 * tile_count // peer_count)
    slot_index = slot_places(target, capacity, peer_count)
    packed = jnp.concatenate([tile_sum, tile_sq], axis=1)
    outgoing = (
        jnp.zeros((peer_count * capacity, 2 * local_cols), jnp.float32).at[slot_index].set(packed)
    )
    labels = (
        jnp.full((peer_count * capacity,), -1.0, jnp.float32)
        .at[slot_index]
        .set(subgroup.astype(jnp.float32))
    )
    arrived, arrived_labels = tuple(
        (
            part.astype(jnp.float32)
            for part in side_by_side(
                (outgoing.astype(jnp.bfloat16), labels.astype(jnp.bfloat16)), "shuf", 0, 0, 1
            )
        )
    )
    group_ids = arrived_labels.astype(jnp.int32)
    members = (group_ids[:, None] == jnp.arange(GRP_DEV, dtype=jnp.int32)[None, :]).astype(
        jnp.float32
    )
    group_sum = jnp.dot(members.T, arrived[:, :local_cols])
    group_sq = jnp.dot(members.T, arrived[:, local_cols:])
    count = float(tile_rows) * jnp.sum(members, axis=0)
    center, inverse = moments(group_sum, group_sq, count, mean_all, square_all)
    slot_center = jnp.dot(members, center)
    slot_inverse = jnp.dot(members, inverse)
    back_center, back_inverse = tuple(
        (
            part.astype(jnp.float32)
            for part in in_one_piece(
                (slot_center.astype(jnp.bfloat16), slot_inverse.astype(jnp.bfloat16)),
                "shuf",
                0,
                0,
                1,
            )
        )
    )
    tile_center = back_center[slot_index]
    tile_scale = back_inverse[slot_index] * col_gain
    scored = ((widened - tile_center[:, None, :]) * tile_scale[:, None, :] + col_bias).astype(
        jnp.bfloat16
    )
    standard = scored.reshape(local_rows, local_cols)
    full_rows = lax.all_to_all(standard, "rep", split_axis=0, concat_axis=1, tiled=True)
    full_weight = gathered_copies(out_weight, "rep", 0)
    summed = jnp.zeros((full_rows.shape[0], full_weight.shape[1]), jnp.float32)
    for block in range(lax.axis_size("rep")):
        partial_value = jnp.dot(
            full_rows[:, block * local_cols : (block + 1) * local_cols],
            full_weight[block * local_cols : (block + 1) * local_cols],
            preferred_element_type=jnp.float32,
        )
        summed = summed + partial_value.astype(jnp.bfloat16).astype(jnp.float32)
    return summed.astype(jnp.bfloat16)


def solution(mesh):
    return jax.shard_map(
        on_device,
        mesh=mesh,
        in_specs=(P("shuf", "rep"), P("shuf"), P("shuf", None), P("rep"), P("rep"), P("rep", None)),
        out_specs=P(("shuf", "rep"), None),
        check_vma=False,
    )
```

profile of v0, /device:TPU:32, one launch (start us, length us, event | category | flops | bytes accessed | tf_op | source)
XLA Modules:
  0.0 160.4 jit_solution(14804359981047646363)
XLA Ops:
  0.0 0.0 copy-start.5
  0.0 0.0 copy-start.2
  0.0 3.3 %convert_reduce_fusion = (f32[256]{0:T(256)S(1)}, f32[256]{0:T(256)S(1)}) fusion(bf16[8192,256]{1,0:T(8,128)(2,1)} %param.6), kind=kLoop, calls=%fused_computation.11 | loop fusion | flops 8388096 | bytes 4196352 | tf_op jit(solution)/shard_map/reduce_sum | solution.py:93
  3.4 0.7 broadcast_in_dim.10
  4.1 11.8 %all-to-all-start.1 = ((f32[64,1,512]{2,1,0:T(1,128)}), f32[64,1,512]{2,1,0:T(1,128)S(1)}, u32[]{:S(2)}, u32[]{:S(2)}) async-start(f32[64,1,512]{2,1,0:T(1,128)} %broadcast_in_dim.10), calls=%async_computation.1 | async-start | bytes 262144 | tf_op jit(solution)/shard_map/all_to_all | solution.py:13
  15.8 0.0 copy-start.3
  15.8 0.0 copy-start.4
  15.9 4.6 %bitcast_reduce_fusion = (f32[64,256]{1,0:T(8,128)S(1)}, f32[64,256]{1,0:T(8,128)S(1)}) fusion(bf16[8192,256]{1,0:T(8,128)(2,1)} %param.6), kind=kLoop, calls=%fused_computation.9 | loop fusion | flops 8355840 | bytes 4325376 | tf_op jit(solution)/shard_map/reduce_sum | solution.py:91
  20.5 0.0 copy-done.5
  20.5 0.0 copy-done.2
  20.5 0.1 fusion.25
  20.6 0.1 reduce_window_sum.11
  20.7 0.2 select_reduce_fusion
  20.9 0.8 scatter_custom_fusion.1
  21.7 0.2 concatenate.23
  21.9 0.9 scatter_custom_fusion
  22.8 0.1 concatenate.18
  22.9 0.8 pad_maximum_fusion
  23.7 2.1 %all-to-all-done.1 = f32[64,1,512]{2,1,0:T(1,128)S(1)} async-done(((f32[64,1,512]{2,1,0:T(1,128)}), f32[64,1,512]{2,1,0:T(1,128)S(1)}, u32[]{:S(2)}, u32[]{:S(2)}) %all-to-all-start.1) | async-done | bytes 131104 | tf_op jit(solution)/shard_map/all_to_all | solution.py:13
  25.9 8.2 %all-to-all-start = ((bf16[64,2,513]{2,1,0:T(2,128)(2,1)}), bf16[64,2,513]{2,1,0:T(2,128)(2,1)S(1)}, u32[]{:S(2)}, u32[]{:S(2)}) async-start(bf16[64,2,513]{2,1,0:T(2,128)(2,1)} %pad_maximum_fusion), calls=%async_computation | async-start | bytes 327680 | tf_op jit(solution)/shard_map/all_to_all | solution.py:37
  34.1 0.1 reduce_sum.71
  34.2 10.3 %all-to-all-done = bf16[64,2,513]{2,1,0:T(2,128)(2,1)S(1)} async-done(((bf16[64,2,513]{2,1,0:T(2,128)(2,1)}), bf16[64,2,513]{2,1,0:T(2,128)(2,1)S(1)}, u32[]{:S(2)}, u32[]{:S(2)}) %all-to-all-start) | async-done | bytes 131360 | tf_op jit(solution)/shard_map/all_to_all | solution.py:37
  44.5 0.1 all_to_all.36
  44.6 0.1 convert_reduce_fusion.1
  44.8 0.1 convert_reduce_fusion.2
  44.9 0.1 fusion.8
  45.0 0.2 convolution_convert_fusion.1
  45.3 0.3 convolution_convert_fusion
  45.6 0.7 all_to_all.38
  46.3 5.5 %all-to-all-start.2 = ((bf16[64,2,512]{2,1,0:T(2,128)(2,1)}), bf16[64,2,512]{2,1,0:T(2,128)(2,1)S(1)}, u32[]{:S(2)}, u32[]{:S(2)}) async-start(bf16[64,2,512]{2,1,0:T(2,128)(2,1)} %all_to_all.38), calls=%async_computation.2 | async-start | bytes 262144 | tf_op jit(solution)/shard_map/all_to_all | solution.py:52
  51.8 10.0 %all-to-all-done.2 = bf16[64,2,512]{2,1,0:T(2,128)(2,1)S(1)} async-done(((bf16[64,2,512]{2,1,0:T(2,128)(2,1)}), bf16[64,2,512]{2,1,0:T(2,128)(2,1)S(1)}, u32[]{:S(2)}, u32[]{:S(2)}) %all-to-all-start.2) | async-done | bytes 131104 | tf_op jit(solution)/shard_map/all_to_all | solution.py:52
  61.8 0.1 all_to_all.40
  61.9 0.7 gather_fusion
  62.5 0.7 gather_fusion.1
  63.2 0.0 copy-done.3
  63.2 0.0 copy-done.4
  63.2 3.6 %fusion.1 = bf16[8192,256]{1,0:T(8,128)(2,1)S(1)} fusion(bf16[8192,256]{1,0:T(8,128)(2,1)} %param.6, f32[256]{0:T(256)S(1)} %copy-done.4, f32[64,256]{1,0:T(8,128)S(1)} %broadcast_multiply_fusion, f32[64,256]{1,0:T(8,128)S(1)} %gather_fusion), kind=kLoop, calls=%fused_computation.6 | loop fusion | flops 10485760 | bytes 8520704 | tf_op jit(solution)/shard_map/convert_element_type | solution.py:141
  66.8 0.0 copy-start.1
  66.8 53.4 %all_to_all.51 = bf16[4,2048,256]{2,1,0:T(8,128)(2,1)} all-to-all(bf16[4,2048,256]{2,1,0:T(8,128)(2,1)S(1)} %bitcast.45), channel_id=1, replica_groups=mesh['shuf'=64,'rep'=4] {'rep'}, dimensions={0} | all-to-all | bytes 8388608 | tf_op jit(solution)/shard_map/all_to_all | solution.py:145
  120.2 0.0 copy-done.1
  120.2 1.6 %broadcast_in_dim.11 = bf16[4,256,1024]{2,1,0:T(8,128)(2,1)} broadcast(bf16[256,1024]{1,0:T(8,128)(2,1)S(1)} %copy-done.1), dimensions={1,2} | broadcast | bytes 2621440 | tf_op jit(solution)/shard_map/broadcast_in_dim | solution.py:14
  121.8 3.8 %all-to-all-start.4 = ((bf16[4,256,1024]{2,1,0:T(8,128)(2,1)}), bf16[4,256,1024]{2,1,0:T(8,128)(2,1)S(1)}, u32[]{:S(2)}, u32[]{:S(2)}) async-start(bf16[4,256,1024]{2,1,0:T(8,128)(2,1)} %broadcast_in_dim.11), calls=%async_computation.4 | async-start | bytes 4194304 | tf_op jit(solution)/shard_map/all_to_all | solution.py:13
  125.6 6.2 %copy.14 = bf16[2048,4,256]{0,2,1:T(8,128)(2,1)} copy(bf16[2048,4,256]{2,0,1:T(8,128)(2,1)} %bitcast.44) | data formatting | bytes 8388608 | tf_op jit(solution)/shard_map/all_to_all | solution.py:145
  131.8 19.0 %all-to-all-done.4 = bf16[4,256,1024]{2,1,0:T(8,128)(2,1)S(1)} async-done(((bf16[4,256,1024]{2,1,0:T(8,128)(2,1)}), bf16[4,256,1024]{2,1,0:T(8,128)(2,1)S(1)}, u32[]{:S(2)}, u32[]{:S(2)}) %all-to-all-start.4) | async-done | bytes 2097184 | tf_op jit(solution)/shard_map/all_to_all | solution.py:13
  150.9 0.0 copy-start
  150.9 2.7 %fusion.10 = bf16[2048,1024]{1,0:T(8,128)(2,1)S(1)} fusion(bf16[2048,1024]{0,1:T(8,128)(2,1)} %bitcast.40, bf16[4,256,1024]{2,1,0:T(8,128)(2,1)S(1)} %all-to-all-done.4), kind=kOutput, calls=%fused_computation.25 | convolution fusion | flops 1073741824 | bytes 5767168 | tf_op jit(solution)/shard_map/dot_general | solution.py:149
  153.5 0.0 copy-done
  153.5 1.3 fusion.12
  154.8 1.3 fusion.14
  156.2 4.3 %add_convert_fusion = bf16[2048,1024]{1,0:T(8,128)(2,1)} fusion(bf16[2048,1024]{1,0:T(8,128)(2,1)S(1)} %fusion.10, bf16[2048,1024]{1,0:T(8,128)(2,1)S(1)} %fusion.12, bf16[2048,1024]{1,0:T(8,128)(2,1)S(1)} %fusion.14, bf16[2048,1024]{0,1:T(8,128)(2,1)S(1)} %bitcast.43, bf16[4,256,1024]{2,1,0:T(8,128)(2,1)S(1)} %all-to-all-done.4), kind=kOutput, calls=%fused_computation.14 | convolution fusion | flops 1092616192 | bytes 18350080 | tf_op jit(solution)/shard_map/dot_general | solution.py:149
  (11 shorter events, 0.1 us)
Async XLA Ops:
  0.0 20.5 %copy-start.5 = (s32[64]{0:T(128)S(1)}, s32[64]{0:T(128)}, u32[]{:S(2)}) copy-start(s32[64]{0:T(128)} %param.7) | copy-start | bytes 772
  0.0 20.5 %copy-start.2 = (s32[64,1]{0,1:T(1,128)S(1)}, s32[64,1]{0,1:T(1,128)}, u32[]{:S(2)}) copy-start(s32[64,1]{0,1:T(1,128)} %param.8) | copy-start | bytes 772
  4.1 21.8 %all-to-all-start.1 = ((f32[64,1,512]{2,1,0:T(1,128)}), f32[64,1,512]{2,1,0:T(1,128)S(1)}, u32[]{:S(2)}, u32[]{:S(2)}) async-start(f32[64,1,512]{2,1,0:T(1,128)} %broadcast_in_dim.10), calls=%async_computation.1 | async-start | bytes 262144 | tf_op jit(solution)/shard_map/all_to_all | solution.py:13
  15.8 47.4 %copy-start.3 = (f32[256]{0:T(256)S(1)}, f32[256]{0:T(256)}, u32[]{:S(2)}) copy-start(f32[256]{0:T(256)} %param.9) | copy-start | bytes 3076
  15.8 47.4 %copy-start.4 = (f32[256]{0:T(256)S(1)}, f32[256]{0:T(256)}, u32[]{:S(2)}) copy-start(f32[256]{0:T(256)} %param.10) | copy-start | bytes 3076
  25.9 18.7 %all-to-all-start = ((bf16[64,2,513]{2,1,0:T(2,128)(2,1)}), bf16[64,2,513]{2,1,0:T(2,128)(2,1)S(1)}, u32[]{:S(2)}, u32[]{:S(2)}) async-start(bf16[64,2,513]{2,1,0:T(2,128)(2,1)} %pad_maximum_fusion), calls=%async_computation | async-start | bytes 327680 | tf_op jit(solution)/shard_map/all_to_all | solution.py:37
  46.3 15.5 %all-to-all-start.2 = ((bf16[64,2,512]{2,1,0:T(2,128)(2,1)}), bf16[64,2,512]{2,1,0:T(2,128)(2,1)S(1)}, u32[]{:S(2)}, u32[]{:S(2)}) async-start(bf16[64,2,512]{2,1,0:T(2,128)(2,1)} %all_to_all.38), calls=%async_computation.2 | async-start | bytes 262144 | tf_op jit(solution)/shard_map/all_to_all | solution.py:52
  66.8 53.4 %copy-start.1 = (bf16[256,1024]{1,0:T(8,128)(2,1)S(1)}, bf16[256,1024]{1,0:T(8,128)(2,1)}, u32[]{:S(2)}) copy-start(bf16[256,1024]{1,0:T(8,128)(2,1)} %param.11) | copy-start | bytes 1572868
  121.8 29.0 %all-to-all-start.4 = ((bf16[4,256,1024]{2,1,0:T(8,128)(2,1)}), bf16[4,256,1024]{2,1,0:T(8,128)(2,1)S(1)}, u32[]{:S(2)}, u32[]{:S(2)}) async-start(bf16[4,256,1024]{2,1,0:T(8,128)(2,1)} %broadcast_in_dim.11), calls=%async_computation.4 | async-start | bytes 4194304 | tf_op jit(solution)/shard_map/all_to_all | solution.py:13
  150.9 2.7 %copy-start = (bf16[2048,4,256]{0,2,1:T(8,128)(2,1)S(1)}, bf16[2048,4,256]{0,2,1:T(8,128)(2,1)}, u32[]{:S(2)}) copy-start(bf16[2048,4,256]{0,2,1:T(8,128)(2,1)} %copy.14) | copy-start | bytes 12582916
where the time goes:
time: 161 us; the launch traced here: 160 us
  blocking collectives  53.4 us (33%)
  waiting for transfers between devices  41.5 us (26%)
  starting transfers between devices  29.2 us (18%)
  other arithmetic  14 us (9%)
  local copies, waits for them, and re-layouts  11.8 us (7%)
  matrix products  10.2 us (6%)
    all_to_all x1, blocking collectives, on_device(): lax.all_to_all(standard, 'rep', split_axis=0, concat_axis=1, tiled=True)  53.4 us
    all_to_all x2, waiting for transfers between devices, from_everyone(): lax.all_to_all(jnp.broadcast_to(value[None], (peers, *value.shape)), axis...  21.2 us
    all_to_all x2, starting transfers between devices, from_everyone(): lax.all_to_all(jnp.broadcast_to(value[None], (peers, *value.shape)), axis...  15.5 us
    all_to_all x1, waiting for transfers between devices, side_by_side(): lax.all_to_all(both, axis, split_axis=split_dim, concat_axis=concat_dim,...  10.3 us
    all_to_all x1, waiting for transfers between devices, in_one_piece(): lax.all_to_all(both, axis, split_axis=split_dim, concat_axis=concat_dim,...  10 us
    dot_general x4, matrix products, on_device(): jnp.dot(full_rows[:, block * local_cols:(block + 1) * local_cols], full_w...  9.54 us
    all_to_all x1, starting transfers between devices, side_by_side(): lax.all_to_all(both, axis, split_axis=split_dim, concat_axis=concat_dim,...  8.21 us
    all_to_all x1, local copies, waits for them, and re-layouts, on_device(): lax.all_to_all(standard, 'rep', split_axis=0, concat_axis=1, tiled=True)  6.2 us
  transfers between devices with their start and end apart: 4, of which 4 were waited for; matrix products, arithmetic and copies ran while one was open for 9% of the time, Pallas kernels for 0%

commit v1 on v0

--- a/solution.py
+++ b/solution.py
@@ -142,7 +142,10 @@
         jnp.bfloat16
     )
     standard = scored.reshape(local_rows, local_cols)
-    full_rows = lax.all_to_all(standard, "rep", split_axis=0, concat_axis=1, tiled=True)
+    full_rows = jnp.concatenate(
+        lax.all_to_all(jnp.stack(jnp.split(standard, lax.axis_size("rep"), axis=0)), "rep", 0, 0),
+        axis=1,
+    )
     full_weight = gathered_copies(out_weight, "rep", 0)
     summed = jnp.zeros((full_rows.shape[0], full_weight.shape[1]), jnp.float32)
     for block in range(lax.axis_size("rep")):

time: 161 us -> 155 us (0.963)
  waiting for transfers between devices: 41.5 us -> 17.8 us
  local copies, waits for them, and re-layouts: 11.8 us -> 23.2 us
  other arithmetic: 14 us -> 22.7 us
    all_to_all x2, waiting for transfers between devices: 21.2 us -> 4.6 us  [from_everyone(): lax.all_to_all(jnp.broadcast_to(value[None], (peers, *value.shape)), axis...]
    another operation x0 -> x4, local copies, waits for them, and re-layouts: none -> 8.2 us  [on_device(): jnp.stack(jnp.split(standard, lax.axis_size('rep'), axis=0))]
    all_to_all x1, waiting for transfers between devices: 10 us -> 2.91 us  [in_one_piece(): lax.all_to_all(both, axis, split_axis=split_dim, concat_axis=concat_dim,...]
    convert_element_type x0 -> x1, local copies, waits for them, and re-layouts: none -> 7.08 us  [on_device(): widened = shaped.astype(jnp.float32)]
    all_to_all x1 -> x0, local copies, waits for them, and re-layouts: 6.2 us -> none  [on_device(): lax.all_to_all(standard, 'rep', split_axis=0, concat_axis=1, tiled=True)]
    convert_element_type x1, other arithmetic: 3.55 us -> 8.4 us  [on_device(): ((widened - tile_center[:, None, :]) * tile_scale[:, None, :] + col_bias)...]
    another operation x0 -> x1, other arithmetic: none -> 3.79 us  [on_device(): jnp.stack(jnp.split(standard, lax.axis_size('rep'), axis=0))]
    split x0 -> x1, local copies, waits for them, and re-layouts: none -> 2.11 us  [on_device(): jnp.split(standard, lax.axis_size('rep'), axis=0)]
  transfers between devices with their start and end apart: 4 -> 4, of which waited for: 4 -> 4; matrix products, arithmetic and copies ran while one was open for 9% -> 25% of each run, Pallas kernels for 0% -> 0%
where the time goes in v1:
time: 155 us
  blocking collectives  52 us (34%)
  starting transfers between devices  29.7 us (19%)
  local copies, waits for them, and re-layouts  23.2 us (15%)
  other arithmetic  22.7 us (15%)
  waiting for transfers between devices  17.8 us (11%)
  matrix products  8.84 us (6%)
    all_to_all x1, blocking collectives, on_device(): lax.all_to_all(jnp.stack(jnp.split(standard, lax.axis_size('rep'), axis=0...  52 us
    all_to_all x2, starting transfers between devices, from_everyone(): lax.all_to_all(jnp.broadcast_to(value[None], (peers, *value.shape)), axis...  16.1 us
    all_to_all x1, waiting for transfers between devices, side_by_side(): lax.all_to_all(both, axis, split_axis=split_dim, concat_axis=concat_dim,...  10.3 us
    convert_element_type x1, other arithmetic, on_device(): ((widened - tile_center[:, None, :]) * tile_scale[:, None, :] + col_bias)...  8.4 us
    another operation x4, local copies, waits for them, and re-layouts, on_device(): jnp.stack(jnp.split(standard, lax.axis_size('rep'), axis=0))  8.2 us
    dot_general x4, matrix products, on_device(): jnp.dot(full_rows[:, block * local_cols:(block + 1) * local_cols], full_w...  8.19 us
    all_to_all x1, starting transfers between devices, side_by_side(): lax.all_to_all(both, axis, split_axis=split_dim, concat_axis=concat_dim,...  8.19 us
    convert_element_type x1, local copies, waits for them, and re-layouts, on_device(): widened = shaped.astype(jnp.float32)  7.08 us
  transfers between devices with their start and end apart: 4, of which 4 were waited for; matrix products, arithmetic and copies ran while one was open for 25% of the time, Pallas kernels for 0%

profile of v1, /device:TPU:32, one launch (start us, length us, event | category | flops | bytes accessed | tf_op | source)
XLA Modules:
  0.0 154.5 jit_solution(16578201030681381784)
XLA Ops:
  0.0 0.0 copy-start.4
  0.0 0.0 copy-start.1
  0.0 3.3 %convert_reduce_fusion = (f32[256]{0:T(256)S(1)}, f32[256]{0:T(256)S(1)}) fusion(bf16[8192,256]{1,0:T(8,128)(2,1)} %param.6), kind=kLoop, calls=%fused_computation.9 | loop fusion | flops 8388096 | bytes 4196352 | tf_op jit(solution)/shard_map/reduce_sum | solution.py:93
  3.4 0.7 broadcast_in_dim.10
  4.1 11.8 %all-to-all-start.1 = ((f32[64,1,512]{2,1,0:T(1,128)}), f32[64,1,512]{2,1,0:T(1,128)S(1)}, u32[]{:S(2)}, u32[]{:S(2)}) async-start(f32[64,1,512]{2,1,0:T(1,128)} %broadcast_in_dim.10), calls=%async_computation.1 | async-start | bytes 262144 | tf_op jit(solution)/shard_map/all_to_all | solution.py:13
  15.8 4.6 %bitcast_reduce_fusion = (f32[64,256]{1,0:T(8,128)S(1)}, f32[64,256]{1,0:T(8,128)S(1)}) fusion(bf16[8192,256]{1,0:T(8,128)(2,1)} %param.6), kind=kLoop, calls=%fused_computation.65 | loop fusion | flops 8355840 | bytes 4325376 | tf_op jit(solution)/shard_map/reduce_sum | solution.py:91
  20.5 0.0 copy-done.4
  20.5 0.0 copy-done.1
  20.5 0.1 fusion.21
  20.6 0.1 reduce_window_sum.11
  20.7 0.2 select_reduce_fusion
  20.9 0.8 scatter_custom_fusion.1
  21.7 0.2 concatenate.23
  21.9 0.9 scatter_custom_fusion
  22.8 0.1 concatenate.18
  22.9 0.8 pad_maximum_fusion.1
  23.7 2.1 %all-to-all-done.1 = f32[64,1,512]{2,1,0:T(1,128)S(1)} async-done(((f32[64,1,512]{2,1,0:T(1,128)}), f32[64,1,512]{2,1,0:T(1,128)S(1)}, u32[]{:S(2)}, u32[]{:S(2)}) %all-to-all-start.1) | async-done | bytes 131104 | tf_op jit(solution)/shard_map/all_to_all | solution.py:13
  25.9 8.2 %all-to-all-start = ((bf16[64,2,513]{2,1,0:T(2,128)(2,1)}), bf16[64,2,513]{2,1,0:T(2,128)(2,1)S(1)}, u32[]{:S(2)}, u32[]{:S(2)}) async-start(bf16[64,2,513]{2,1,0:T(2,128)(2,1)} %pad_maximum_fusion.1), calls=%async_computation | async-start | bytes 327680 | tf_op jit(solution)/shard_map/all_to_all | solution.py:37
  34.0 0.1 reduce_sum.71
  34.2 10.3 %all-to-all-done = bf16[64,2,513]{2,1,0:T(2,128)(2,1)S(1)} async-done(((bf16[64,2,513]{2,1,0:T(2,128)(2,1)}), bf16[64,2,513]{2,1,0:T(2,128)(2,1)S(1)}, u32[]{:S(2)}, u32[]{:S(2)}) %all-to-all-start) | async-done | bytes 131360 | tf_op jit(solution)/shard_map/all_to_all | solution.py:37
  44.5 0.1 all_to_all.25
  44.6 0.1 convert_reduce_fusion.1
  44.7 0.1 convert_reduce_fusion.2
  44.9 0.1 fusion.4
  45.0 0.2 convolution_convert_fusion.1
  45.2 0.3 convolution_convert_fusion
  45.5 0.7 all_to_all.27
  46.3 5.5 %all-to-all-start.2 = ((bf16[64,2,512]{2,1,0:T(2,128)(2,1)}), bf16[64,2,512]{2,1,0:T(2,128)(2,1)S(1)}, u32[]{:S(2)}, u32[]{:S(2)}) async-start(bf16[64,2,512]{2,1,0:T(2,128)(2,1)} %all_to_all.27), calls=%async_computation.2 | async-start | bytes 262144 | tf_op jit(solution)/shard_map/all_to_all | solution.py:52
  51.7 0.0 copy-start
  51.7 7.1 %copy.22 = f32[64,128,256]{1,0,2:T(8,128)} copy(bf16[64,128,256]{2,1,0:T(8,128)(2,1)} %bitcast.37) | data formatting | bytes 12582912 | tf_op jit(solution)/shard_map/convert_element_type | solution.py:90
  58.8 0.0 copy-start.2
  58.8 0.0 copy-start.3
  58.8 2.9 %all-to-all-done.2 = bf16[64,2,512]{2,1,0:T(2,128)(2,1)S(1)} async-done(((bf16[64,2,512]{2,1,0:T(2,128)(2,1)}), bf16[64,2,512]{2,1,0:T(2,128)(2,1)S(1)}, u32[]{:S(2)}, u32[]{:S(2)}) %all-to-all-start.2) | async-done | bytes 131104 | tf_op jit(solution)/shard_map/all_to_all | solution.py:52
  61.8 0.0 copy-done
  61.8 1.7 %broadcast_in_dim.11 = bf16[4,256,1024]{2,1,0:T(8,128)(2,1)} broadcast(bf16[256,1024]{1,0:T(8,128)(2,1)S(1)} %copy-done), dimensions={1,2} | broadcast | bytes 2621440 | tf_op jit(solution)/shard_map/broadcast_in_dim | solution.py:14
  63.4 4.3 %all-to-all-start.4 = ((bf16[4,256,1024]{2,1,0:T(8,128)(2,1)}), bf16[4,256,1024]{2,1,0:T(8,128)(2,1)S(1)}, u32[]{:S(2)}, u32[]{:S(2)}) async-start(bf16[4,256,1024]{2,1,0:T(8,128)(2,1)} %broadcast_in_dim.11), calls=%async_computation.4 | async-start | bytes 4194304 | tf_op jit(solution)/shard_map/all_to_all | solution.py:13
  67.7 0.1 all_to_all.29
  67.8 0.7 gather_fusion
  68.5 0.7 gather_fusion.1
  69.1 0.0 copy-done.2
  69.1 0.1 copy.23
  69.2 0.1 copy.21
  69.3 0.0 copy-done.3
  69.3 8.4 %add_convert_fusion.1 = bf16[64,128,256]{1,0,2:T(8,128)(2,1)S(1)} fusion(f32[64,128,256]{1,0,2:T(8,128)} %copy.22, f32[256]{0:T(256)S(1)} %copy-done.3, f32[64,256]{0,1:T(8,128)S(1)} %copy.23, f32[64,256]{0,1:T(8,128)S(1)} %copy.21), kind=kLoop, calls=%fused_computation.5 | loop fusion | flops 8388608 | bytes 12715008 | tf_op jit(solution)/shard_map/convert_element_type | solution.py:141
  77.8 2.1 %fusion.33 = (bf16[16,128,256]{1,0,2:T(8,128)(2,1)}, bf16[16,128,256]{1,0,2:T(8,128)(2,1)}, bf16[16,128,256]{1,0,2:T(8,128)(2,1)}, bf16[16,128,256]{1,0,2:T(8,128)(2,1)S(1)}) fusion(bf16[64,128,256]{1,0,2:T(8,128)(2,1)S(1)} %add_convert_fusion.1), kind=kLoop, calls=%fused_computation.67 | loop fusion | bytes 8388608 | tf_op jit(solution)/shard_map/split | solution.py:146
  79.9 2.3 %stack.15 = bf16[1,2048,256]{1,2,0:T(8,128)(2,1)} reshape(bf16[16,128,256]{1,0,2:T(8,128)(2,1)} %get-tuple-element.9) | data formatting | bytes 2097152 | tf_op jit(solution)/shard_map/stack | solution.py:146
  82.2 2.3 %stack.18 = bf16[1,2048,256]{1,2,0:T(8,128)(2,1)} reshape(bf16[16,128,256]{1,0,2:T(8,128)(2,1)} %get-tuple-element.10) | data formatting | bytes 2097152 | tf_op jit(solution)/shard_map/stack | solution.py:146
  84.5 2.3 %stack.17 = bf16[1,2048,256]{1,2,0:T(8,128)(2,1)} reshape(bf16[16,128,256]{1,0,2:T(8,128)(2,1)} %get-tuple-element.11) | data formatting | bytes 2097152 | tf_op jit(solution)/shard_map/stack | solution.py:146
  86.8 1.3 stack.16
  88.1 3.8 %pad_maximum_fusion = bf16[4,2048,256]{1,2,0:T(8,128)(2,1)} fusion(bf16[1,2048,256]{1,2,0:T(8,128)(2,1)} %stack.18, bf16[1,2048,256]{1,2,0:T(8,128)(2,1)} %stack.17, bf16[1,2048,256]{1,2,0:T(8,128)(2,1)} %stack.16, bf16[1,2048,256]{1,2,0:T(8,128)(2,1)} %stack.15), kind=kLoop, calls=%fused_computation.8 | loop fusion | flops 6291456 | bytes 8388608 | tf_op jit(solution)/shard_map/stack | solution.py:146
  91.9 2.5 %all-to-all-done.4 = bf16[4,256,1024]{2,1,0:T(8,128)(2,1)S(1)} async-done(((bf16[4,256,1024]{2,1,0:T(8,128)(2,1)}), bf16[4,256,1024]{2,1,0:T(8,128)(2,1)S(1)}, u32[]{:S(2)}, u32[]{:S(2)}) %all-to-all-start.4) | async-done | bytes 2097184 | tf_op jit(solution)/shard_map/all_to_all | solution.py:13
  94.3 52.0 %all_to_all.37 = bf16[4,2048,256]{1,2,0:T(8,128)(2,1)S(1)} all-to-all(bf16[4,2048,256]{1,2,0:T(8,128)(2,1)} %pad_maximum_fusion), channel_id=1, replica_groups=mesh['shuf'=64,'rep'=4] {'rep'}, dimensions={0} | all-to-all | bytes 8388608 | tf_op jit(solution)/shard_map/all_to_all | solution.py:146
  146.3 1.3 fusion.6
  147.6 1.3 fusion.8
  148.9 1.3 fusion.10
  150.2 4.3 %add_convert_fusion = bf16[2048,1024]{1,0:T(8,128)(2,1)} fusion(bf16[2048,1024]{1,0:T(8,128)(2,1)S(1)} %fusion.6, bf16[2048,1024]{1,0:T(8,128)(2,1)S(1)} %fusion.8, bf16[2048,1024]{1,0:T(8,128)(2,1)S(1)} %fusion.10, bf16[2048,1024]{0,1:T(8,128)(2,1)S(1)} %bitcast.41, bf16[4,256,1024]{2,1,0:T(8,128)(2,1)S(1)} %all-to-all-done.4), kind=kOutput, calls=%fused_computation.4 | convolution fusion | flops 1092616192 | bytes 18350080 | tf_op jit(solution)/shard_map/dot_general | solution.py:152
  (11 shorter events, 0.1 us)
Async XLA Ops:
  0.0 20.5 %copy-start.4 = (s32[64]{0:T(128)S(1)}, s32[64]{0:T(128)}, u32[]{:S(2)}) copy-start(s32[64]{0:T(128)} %param.7) | copy-start | bytes 772
  0.0 20.5 %copy-start.1 = (s32[64,1]{0,1:T(1,128)S(1)}, s32[64,1]{0,1:T(1,128)}, u32[]{:S(2)}) copy-start(s32[64,1]{0,1:T(1,128)} %param.8) | copy-start | bytes 772
  4.1 21.8 %all-to-all-start.1 = ((f32[64,1,512]{2,1,0:T(1,128)}), f32[64,1,512]{2,1,0:T(1,128)S(1)}, u32[]{:S(2)}, u32[]{:S(2)}) async-start(f32[64,1,512]{2,1,0:T(1,128)} %broadcast_in_dim.10), calls=%async_computation.1 | async-start | bytes 262144 | tf_op jit(solution)/shard_map/all_to_all | solution.py:13
  25.9 18.6 %all-to-all-start = ((bf16[64,2,513]{2,1,0:T(2,128)(2,1)}), bf16[64,2,513]{2,1,0:T(2,128)(2,1)S(1)}, u32[]{:S(2)}, u32[]{:S(2)}) async-start(bf16[64,2,513]{2,1,0:T(2,128)(2,1)} %pad_maximum_fusion.1), calls=%async_computation | async-start | bytes 327680 | tf_op jit(solution)/shard_map/all_to_all | solution.py:37
  46.3 15.5 %all-to-all-start.2 = ((bf16[64,2,512]{2,1,0:T(2,128)(2,1)}), bf16[64,2,512]{2,1,0:T(2,128)(2,1)S(1)}, u32[]{:S(2)}, u32[]{:S(2)}) async-start(bf16[64,2,512]{2,1,0:T(2,128)(2,1)} %all_to_all.27), calls=%async_computation.2 | async-start | bytes 262144 | tf_op jit(solution)/shard_map/all_to_all | solution.py:52
  51.7 10.0 %copy-start = (bf16[256,1024]{1,0:T(8,128)(2,1)S(1)}, bf16[256,1024]{1,0:T(8,128)(2,1)}, u32[]{:S(2)}) copy-start(bf16[256,1024]{1,0:T(8,128)(2,1)} %param.11) | copy-start | bytes 1572868
  58.8 10.3 %copy-start.2 = (f32[256]{0:T(256)S(1)}, f32[256]{0:T(256)}, u32[]{:S(2)}) copy-start(f32[256]{0:T(256)} %param.9) | copy-start | bytes 3076
  58.8 10.5 %copy-start.3 = (f32[256]{0:T(256)S(1)}, f32[256]{0:T(256)}, u32[]{:S(2)}) copy-start(f32[256]{0:T(256)} %param.10) | copy-start | bytes 3076
  63.4 30.9 %all-to-all-start.4 = ((bf16[4,256,1024]{2,1,0:T(8,128)(2,1)}), bf16[4,256,1024]{2,1,0:T(8,128)(2,1)S(1)}, u32[]{:S(2)}, u32[]{:S(2)}) async-start(bf16[4,256,1024]{2,1,0:T(8,128)(2,1)} %broadcast_in_dim.11), calls=%async_computation.4 | async-start | bytes 4194304 | tf_op jit(solution)/shard_map/all_to_all | solution.py:13
